TPU v7x, 256 devices: a 2x2x32 block of a 4x8x32 slice. The times are simulated.
256 devices in a mesh: grp: 4 (over y, x), panel: 64 (over z, core).
Axes of the slice: x: 2, y: 2, z: 32, core: 2. Of those that a mesh axis runs over, the one named last changes fastest.
The devices are a block of a 4x8x32 slice.
Arguments:
- density: bfloat16 [8192, 16, 128], P(('grp', 'panel')), parts along dimension 0, may hold values from -6 to 6
- near_blocks: bfloat16 [8192, 8, 128, 128], P(('grp', 'panel')), parts along dimension 0, may hold values from -0.1875 to 0.1875
- neighbours: int32 [8192, 8], P(('grp', 'panel')), parts along dimension 0, may hold values from 0 to 2047, as said below
- counts: int32 [8192], P(('grp', 'panel')), parts along dimension 0, may hold values from 1 to 8, as said below
- coarse_map: int32 [8192], P(('grp', 'panel')), parts along dimension 0, may hold values from 0 to 127, as said below
- restrict: bfloat16 [8192, 128, 128], P(('grp', 'panel')), parts along dimension 0, may hold values from -0.125 to 0.125
- evaluate: bfloat16 [8192, 128, 128], P(('grp', 'panel')), parts along dimension 0, may hold values from -0.5 to 0.5
- coupling: float32 [512, 128], P(('grp', 'panel')), parts along dimension 0, as said below
Outputs:
- potential: bfloat16 [8192, 16, 128], P(('grp', 'panel')), parts along dimension 0
There are 4 independent parts, one for each index of `grp`. A program takes and returns all parts, laid end to end along the dimension named above; each array names one. Nothing has to cross between parts.
Inputs may be any that keep to these rules, and one draw needn't show every extreme that they name: `neighbours`: slot 0 of block b is b itself; every entry lies within 16 blocks of b; in every draw some entry lies exactly 16 blocks below its block and some exactly 16 above. `counts`: every device holds blocks with all 8 slots live. `coarse_map`: block b's coarse cluster is one of the 2 clusters from (b // 32) * 2 on. `coupling`: the matrix is symmetric.
All inputs are finite; a program needn't handle non-finite values.
Results may differ from a plain program's by a relative error of at most 0.0042.
Values may be sent and summed in bfloat16 or wider, within the bound.
A program may use at most 64 MiB of HBM per device.

v0:
```python
import functools

import jax
import jax.numpy as jnp
from jax import lax
from jax.experimental import pallas as pl
from jax.experimental.pallas import tpu as pltpu
from jax.sharding import PartitionSpec as P

GRP_PANEL = ("grp", "panel")
MESH = pl.DeviceIdType.MESH
PAIR = 2
URGENT = 2
NT = (((1,), (1,)), ((), ()))
NN = (((1,), (0,)), ((), ()))


def kernel(
    size,
    nbr_hbm,
    cnt_hbm,
    map_hbm,
    cpl_hbm,
    dens_hbm,
    near_hbm,
    res_hbm,
    eva_hbm,
    out_hbm,
    nbr,
    cnt,
    cmap,
    cpl,
    ext,
    near_v,
    res_v,
    eva_v,
    nearf,
    out_v,
    gath,
    own_m,
    cpl_v,
    acc,
    loc,
    loc_out,
    smem_sem,
    dens_sem,
    res_sem,
    near_sem,
    eva_sem,
    out_sem,
    cpl_sem,
    send_sem,
    chunk_sem,
    row_sem,
    halo_sem,
    loc_sem,
):
    chips = size // 2
    second = chips // 4
    relays = [r for r in range(PAIR)] + [second + r for r in range(PAIR)]
    count = len(relays)
    blocks, rhs, width = dens_hbm.shape
    slots = nbr_hbm.shape[0]
    reach = blocks // 2
    me = lax.axis_index("panel")
    chip = me // 2
    core = me % 2
    in_first = chip < PAIR
    in_second = jnp.logical_and(chip >= second, chip < second + PAIR)
    is_relay = jnp.logical_and(core == 1, jnp.logical_or(in_first, in_second))
    served = jnp.where(in_first, second // PAIR, (chips - second) // PAIR) * 2
    base = jnp.where(chip < second, 0, second)
    my_relay = (base + chip % PAIR) * 2 + 1
    place = (chip - base) // PAIR * 2 + core
    has_left = me > 0
    has_right = me < size - 1

    def remote(src, dst, ssem, rsem, device):
        return pltpu.make_async_remote_copy(
            src_ref=src,
            dst_ref=dst,
            send_sem=ssem,
            recv_sem=rsem,
            device_id={"panel": device},
            device_id_type=MESH,
        )

    barrier = pltpu.get_barrier_semaphore()

    def greet(device):
        pl.semaphore_signal(barrier, inc=1, device_id={"panel": device}, device_id_type=MESH)

    @pl.when(has_left)
    def _():
        greet(me - 1)

    @pl.when(has_right)
    def _():
        greet(me + 1)

    own = ext.at[pl.ds(reach, blocks)]
    load_dens = pltpu.make_async_copy(dens_hbm, own, dens_sem)
    load_dens.start()
    parts = 2
    per = blocks // parts
    load_res = []
    for i in range(parts):
        piece = pl.ds(i * per, per)
        cp = pltpu.make_async_copy(res_hbm.at[piece], res_v.at[piece], res_sem.at[i])
        cp.start()
        load_res.append(cp)
    small = [
        pltpu.make_async_copy(map_hbm, cmap, smem_sem.at[0]),
        pltpu.make_async_copy(nbr_hbm, nbr, smem_sem.at[1]),
        pltpu.make_async_copy(cnt_hbm, cnt, smem_sem.at[2]),
    ]
    for cp in small:
        cp.start()

    @pl.when(is_relay)
    def _():
        def body(k, carry):
            greet(lax.rem(me + k, size))
            return carry

        lax.fori_loop(1, size, body, 0)

    pieces = 4
    step = blocks // pieces
    load_near = []
    for i in range(pieces):
        piece = pl.ds(i * step, step)
        load_near.append(
            pltpu.make_async_copy(near_hbm.at[piece], near_v.at[piece], near_sem.at[i])
        )
    load_eva = pltpu.make_async_copy(eva_hbm, eva_v, eva_sem)

    for cp in small:
        cp.wait()
    load_dens.wait()
    total = jnp.zeros((2 * rhs, width), jnp.float32)
    zero = jnp.zeros((rhs, width), jnp.bfloat16)

    def add_moments(total, first, last):
        for b in range(first, last, 2):
            rows = []
            for c in range(2):
                rows.append(
                    jnp.concatenate(
                        [
                            jnp.where(cmap[b + k] == 2 * me + c, ext[reach + b + k], zero)
                            for k in range(2)
                        ],
                        axis=1,
                    )
                )
            lhs = jnp.concatenate(rows, axis=0)
            weights = jnp.concatenate([res_v[b], res_v[b + 1]], axis=1)
            total += lax.dot_general(lhs, weights, NT, preferred_element_type=jnp.float32)
        return total

    low_halo = ext.at[pl.ds(0, reach)]
    high_halo = ext.at[pl.ds(reach + blocks, reach)]
    first_rows = ext.at[pl.ds(reach, reach)]
    last_rows = ext.at[pl.ds(blocks, reach)]
    up = remote(last_rows, low_halo, send_sem.at[count + 1], halo_sem.at[0], me + 1)
    down = remote(first_rows, high_halo, send_sem.at[count + 2], halo_sem.at[1], me - 1)

    load_res[0].wait()
    for cp in load_near[:2]:
        cp.start()
    total = add_moments(total, 0, per)
    pl.semaphore_wait(
        barrier,
        count + has_left.astype(jnp.int32) + has_right.astype(jnp.int32) - is_relay.astype(jnp.int32),
    )
    pl.when(has_right)(up.start)
    pl.when(has_left)(down.start)
    load_res[1].wait()
    total = add_moments(total, per, blocks)
    own_m[...] = total.astype(jnp.bfloat16).reshape(2, rhs, width)
    for cp in load_near[2:]:
        cp.start()
    load_eva.start()

    def to_relay(r):
        device = 2 * relays[r] + 1
        cp = remote(own_m, gath.at[chip, core], send_sem.at[r], chunk_sem.at[chip, core], device)
        return me != device, cp

    def send_to(which):
        for r in which:
            other, cp = to_relay(r)
            pl.when(other)(cp.start)

    send_to(range(PAIR))
    rows_to = remote(cpl_hbm, cpl_v.at[place], send_sem.at[count], row_sem.at[place], my_relay)
    pl.when(jnp.logical_not(is_relay))(rows_to.start)

    def prepare():
        gath[chip, 1] = own_m[...]
        acc[...] = jnp.zeros(acc.shape, jnp.float32)
        mine = pltpu.make_async_copy(cpl_hbm, cpl_v.at[place], cpl_sem)
        mine.start()

        def row_body(k, carry):
            at = lax.rem(place + k, served)
            remote(cpl_v.at[at], cpl_v.at[at], send_sem.at[0], row_sem.at[at], me).wait_recv()
            return carry

        lax.fori_loop(1, served, row_body, 0)
        mine.wait()
        table = pltpu.make_async_copy(cpl_v, cpl, cpl_sem)
        table.start()
        table.wait()

    @pl.when(jnp.logical_and(is_relay, in_first))
    def _():
        prepare()

    for cp in load_near:
        cp.wait()

    @pl.when(has_left)
    def _():
        up.wait_recv()

    @pl.when(has_right)
    def _():
        down.wait_recv()

    @pl.when(jnp.logical_not(has_left))
    def _():
        ext[pl.ds(0, reach)] = jnp.zeros((reach, rhs, width), jnp.bfloat16)

    @pl.when(jnp.logical_not(has_right))
    def _():
        ext[pl.ds(reach + blocks, reach)] = jnp.zeros((reach, rhs, width), jnp.bfloat16)

    def near_block(b, carry):
        picked = []
        for j in range(slots):
            where = nbr[j, b] - (me * blocks - reach)
            where = jnp.minimum(jnp.maximum(where, 0), 2 * blocks - 1)
            picked.append(jnp.where(j < cnt[b], ext[where], zero))
        value = jnp.zeros((rhs, width), jnp.float32)
        for j in range(0, slots, 2):
            lhs = jnp.concatenate([picked[j], picked[j + 1]], axis=1)
            weights = jnp.concatenate([near_v[b, j], near_v[b, j + 1]], axis=1)
            value += lax.dot_general(lhs, weights, NT, preferred_element_type=jnp.float32)
        nearf[b] = value
        return carry

    lax.fori_loop(0, blocks, near_block, 0, unroll=2)
    send_to(range(PAIR, count))

    @pl.when(jnp.logical_and(is_relay, in_second))
    def _():
        prepare()

    for r in range(count):
        other, cp = to_relay(r)
        pl.when(other)(cp.wait_send)
    pl.when(jnp.logical_not(is_relay))(rows_to.wait_send)
    pl.when(has_right)(up.wait_send)
    pl.when(has_left)(down.wait_send)
    load_eva.wait()

    store = pltpu.make_async_copy(out_v, out_hbm, out_sem)

    def finish(one, two):
        for b in range(blocks):
            lhs = jnp.where(cmap[b] == 2 * me, one, two)
            far = lax.dot_general(lhs, eva_v[b], NN, preferred_element_type=jnp.float32)
            out_v[b] = (nearf[b] + far).astype(jnp.bfloat16)
        store.start()

    @pl.when(jnp.logical_not(is_relay))
    def _():
        remote(loc, loc, send_sem.at[0], loc_sem, me).wait_recv()
        finish(loc[0], loc[1])
        store.wait()

    @pl.when(is_relay)
    def _():
        def arrive(slot, which):
            ref = gath.at[slot, which]
            remote(ref, ref, send_sem.at[0], chunk_sem.at[slot, which], me).wait_recv()

        def moments_of(slot):
            return [gath[slot, q // 2, q % 2].astype(jnp.float32) for q in range(4)]

        def add(at, slot, moments):
            values = []
            for c in range(2):
                value = acc[at, c]
                for q in range(4):
                    value += cpl[at, c, 4 * slot + q] * moments[q]
                values.append(value)
            return values

        def take(slot):
            moments = moments_of(slot)

            def inner(k, carry):
                for at in [8 * k + n for n in range(8)]:
                    values = add(at, slot, moments)
                    acc[at, 0] = values[0]
                    acc[at, 1] = values[1]
                return carry

            lax.fori_loop(0, served // 8, inner, 0)

        arrive(chip, 0)
        take(chip)

        def both(d, carry):
            for sign in (1, -1):
                slot = lax.rem(chip + sign * d + chips, chips)
                for which in (0, 1):
                    arrive(slot, which)
                take(slot)
            return carry

        lax.fori_loop(1, chips // 2, both, 0)
        last = lax.rem(chip + chips // 2, chips)
        for which in (0, 1):
            arrive(last, which)
        moments = moments_of(last)

        def result(at):
            values = add(at, last, moments)
            for c in range(2):
                loc_out[at, c] = values[c].astype(jnp.bfloat16)

        def give(at):
            device = (at // 2 * PAIR + chip) * 2 + at % 2
            return remote(loc_out.at[at], loc, send_sem.at[count + 3 + at], loc_sem, device)

        result(0)
        give(0).start()
        result(1)
        for at in range(2, 2 * URGENT):
            result(at)
            give(at).start()
        finish(loc_out[1, 0], loc_out[1, 1])

        def rest(at, carry):
            result(at)
            give(at).start()
            return carry

        lax.fori_loop(2 * URGENT, served, rest, 0)
        store.wait()

        def sent(at, carry):
            give(at).wait_send()
            return carry

        give(0).wait_send()
        lax.fori_loop(2, served, sent, 0)


def shards(size, density, near_blocks, neighbours, counts, coarse_map, restrict, evaluate, coupling):
    blocks, rhs, width = density.shape
    slots = neighbours.shape[1]
    terms = restrict.shape[1]
    chips = size // 2
    served = 2 * (chips - chips // 4) // PAIR
    count = 2 * PAIR
    bf16, f32 = jnp.bfloat16, jnp.float32
    dma = pltpu.SemaphoreType.DMA
    anywhere = pl.BlockSpec(memory_space=pl.ANY)
    return pl.pallas_call(
        functools.partial(kernel, size),
        out_shape=jax.ShapeDtypeStruct(density.shape, bf16),
        in_specs=[anywhere] * 8,
        out_specs=anywhere,
        scratch_shapes=[
            pltpu.SMEM((slots, blocks), jnp.int32),
            pltpu.SMEM((blocks,), jnp.int32),
            pltpu.SMEM((blocks,), jnp.int32),
            pltpu.SMEM((served, 2, 2 * size), f32),
            pltpu.VMEM((2 * blocks, rhs, width), bf16),
            pltpu.VMEM(near_blocks.shape, bf16),
            pltpu.VMEM(restrict.shape, bf16),
            pltpu.VMEM(evaluate.shape, bf16),
            pltpu.VMEM((blocks, rhs, width), f32),
            pltpu.VMEM((blocks, rhs, width), bf16),
            pltpu.VMEM((chips, 2, 2, rhs, terms), bf16),
            pltpu.VMEM((2, rhs, terms), bf16),
            pltpu.VMEM((served, 2, 2 * size), f32),
            pltpu.VMEM((served, 2, rhs, terms), f32),
            pltpu.VMEM((2, rhs, terms), bf16),
            pltpu.VMEM((served, 2, rhs, terms), bf16),
            dma((3,)),
            dma,
            dma((2,)),
            dma((4,)),
            dma,
            dma,
            dma,
            dma((count + 3 + served,)),
            dma((chips, 2)),
            dma((served,)),
            dma((2,)),
            dma,
        ],
        compiler_params=pltpu.CompilerParams(
            collective_id=0, has_side_effects=True, vmem_limit_bytes=67043328
        ),
        name="operator",
    )(neighbours.T, counts, coarse_map, coupling, density, near_blocks, restrict, evaluate)


def solution(mesh):
    placed = (
        P(GRP_PANEL, None, None),
        P(GRP_PANEL, None, None, None),
        P(GRP_PANEL, None),
        P(GRP_PANEL),
        P(GRP_PANEL),
        P(GRP_PANEL, None, None),
        P(GRP_PANEL, None, None),
        P(GRP_PANEL, None),
    )
    return jax.shard_map(
        functools.partial(shards, mesh.shape["panel"]),
        mesh=mesh,
        in_specs=placed,
        out_specs=P(GRP_PANEL, None, None),
        check_vma=False,
    )
```

profile of v0, /device:TPU:37, one launch (start us, length us, event | category | flops | bytes accessed | tf_op | source)
XLA Modules:
  0.0 39.3 jit_solution(617391592350873058)
XLA Ops:
  0.0 37.7 %operator.1 = bf16[32,16,128]{2,1,0:T(8,128)(2,1)} custom-call(s32[8,32]{1,0:T(8,128)} %bitcast.1, s32[32]{0:T(128)} %cnt_hbm.1, s32[32]{0:T(128)} %map_hbm.1, f32[2,128]{1,0:T(2,128)} %cpl_hbm.1, bf16[32,16,128]{2,1,0:T(8,128)(2,1)} %dens_hbm.1, bf16[32,8,128,128]{3,2,1,0:T(8,128)(2,1)} %near_hbm.1, bf16[32,128,128]{2,1,0:T(8,128)(2,1)} %res_hbm.1, ...), custom_call_target="tpu_custom_call" | custom-call | tf_op jit(solution)/shard_map/operator/pallas_call | solution.py:374
  37.7 1.6 %copy.10 = bf16[32,16,128]{2,1,0:T(8,128)(2,1)} copy(bf16[32,16,128]{2,1,0:T(8,128)(2,1)} %operator.1) | data formatting | bytes 262144
where the time goes:
time: 39.8 us; the launch traced here: 39.3 us
  Pallas kernels  37.7 us (95%)
  local copies, waits for them, and re-layouts  1.57 us (4%)
    pallas_call x1, Pallas kernels, shards(): pl.pallas_call(functools.partial(kernel, size), out_shape=jax.ShapeDtypeS...  37.7 us
    unnamed x1, local copies, waits for them, and re-layouts  1.57 us

commit v1 on v0

v1 whole, which is shorter than its diff:
```python
import functools

import jax
import jax.numpy as jnp
from jax import lax
from jax.experimental import pallas as pl
from jax.experimental.pallas import tpu as pltpu
from jax.sharding import PartitionSpec as P

GRP_PANEL = ("grp", "panel")
MESH = pl.DeviceIdType.MESH
FIRST = 2
SECOND = 3
AT = 8
NT = (((1,), (1,)), ((), ()))
NN = (((1,), (0,)), ((), ()))


def kernel(
    size,
    nbr_hbm,
    cnt_hbm,
    map_hbm,
    cpl_hbm,
    dens_hbm,
    near_hbm,
    res_hbm,
    eva_hbm,
    out_hbm,
    nbr,
    cnt,
    cmap,
    cpl,
    ext,
    near_v,
    res_v,
    eva_v,
    nearf,
    out_v,
    gath,
    own_m,
    own_rows,
    cpl_v,
    acc,
    loc,
    loc_out,
    smem_sem,
    dens_sem,
    res_sem,
    near_sem,
    eva_sem,
    out_sem,
    cpl_sem,
    send_sem,
    chunk_sem,
    row_sem,
    halo_sem,
    loc_sem,
    result_sem,
):
    chips = size // 2
    second = chips // 4
    relays = [r for r in range(FIRST)] + [second + r for r in range(SECOND)]
    count = len(relays)
    blocks, rhs, width = dens_hbm.shape
    slots = nbr_hbm.shape[0]
    reach = blocks // 2
    me = lax.axis_index("panel")
    chip = me // 2
    core = me % 2
    in_first = chip < FIRST
    in_second = jnp.logical_and(chip >= second, chip < second + SECOND)
    is_relay = jnp.logical_and(core == 1, jnp.logical_or(in_first, in_second))
    first_served = 2 * (second // FIRST)
    second_served = 2 * ((chips - second) // SECOND)
    served = jnp.where(in_first, first_served, second_served)
    base = jnp.where(chip < second, 0, second)
    stride = jnp.where(chip < second, FIRST, SECOND)
    my_relay = (base + lax.rem(chip - base, stride)) * 2 + 1
    place = lax.div(chip - base, stride) * 2 + core
    has_left = me > 0
    has_right = me < size - 1

    def remote(src, dst, ssem, rsem, device):
        return pltpu.make_async_remote_copy(
            src_ref=src,
            dst_ref=dst,
            send_sem=ssem,
            recv_sem=rsem,
            device_id={"panel": device},
            device_id_type=MESH,
        )

    barrier = pltpu.get_barrier_semaphore()

    def greet(device):
        pl.semaphore_signal(barrier, inc=1, device_id={"panel": device}, device_id_type=MESH)

    @pl.when(has_left)
    def _():
        greet(me - 1)

    @pl.when(has_right)
    def _():
        greet(me + 1)

    own = ext.at[pl.ds(reach, blocks)]
    load_dens = pltpu.make_async_copy(dens_hbm, own, dens_sem)
    load_dens.start()
    parts = 2
    per = blocks // parts
    load_res = []
    for i in range(parts):
        piece = pl.ds(i * per, per)
        cp = pltpu.make_async_copy(res_hbm.at[piece], res_v.at[piece], res_sem.at[i])
        cp.start()
        load_res.append(cp)
    small = [
        pltpu.make_async_copy(map_hbm, cmap, smem_sem.at[0]),
        pltpu.make_async_copy(nbr_hbm, nbr, smem_sem.at[1]),
        pltpu.make_async_copy(cnt_hbm, cnt, smem_sem.at[2]),
        pltpu.make_async_copy(cpl_hbm, own_rows, smem_sem.at[3]),
    ]
    for cp in small:
        cp.start()

    @pl.when(is_relay)
    def _():
        def body(k, carry):
            greet(lax.rem(me + k, size))
            return carry

        lax.fori_loop(1, size, body, 0)

    pieces = 4
    step = blocks // pieces
    load_near = []
    for i in range(pieces):
        piece = pl.ds(i * step, step)
        load_near.append(
            pltpu.make_async_copy(near_hbm.at[piece], near_v.at[piece], near_sem)
        )
    load_eva = pltpu.make_async_copy(eva_hbm, eva_v, eva_sem)

    for cp in small:
        cp.wait()
    load_dens.wait()
    total = jnp.zeros((2 * rhs, width), jnp.float32)
    zero = jnp.zeros((rhs, width), jnp.bfloat16)

    def add_moments(total, first, last):
        rows = []
        for c in range(2):
            rows.append(
                jnp.concatenate(
                    [jnp.where(cmap[b] == 2 * me + c, ext[reach + b], zero) for b in range(first, last)],
                    axis=1,
                )
            )
        lhs = jnp.concatenate(rows, axis=0)
        weights = jnp.concatenate([res_v[b] for b in range(first, last)], axis=1)
        total += lax.dot_general(lhs, weights, NT, preferred_element_type=jnp.float32)
        return total

    low_halo = ext.at[pl.ds(0, reach)]
    high_halo = ext.at[pl.ds(reach + blocks, reach)]
    first_rows = ext.at[pl.ds(reach, reach)]
    last_rows = ext.at[pl.ds(blocks, reach)]
    up = remote(last_rows, low_halo, send_sem.at[count + 1], halo_sem.at[0], me + 1)
    down = remote(first_rows, high_halo, send_sem.at[count + 2], halo_sem.at[1], me - 1)

    load_res[0].wait()
    for cp in load_near[:2]:
        cp.start()
    total = add_moments(total, 0, per)
    load_res[1].wait()
    total = add_moments(total, per, blocks)
    own_m[...] = total.astype(jnp.bfloat16).reshape(2, rhs, width)
    for cp in load_near[2:]:
        cp.start()
    load_eva.start()

    def to_relay(r):
        device = 2 * relays[r] + 1
        ahead = lax.rem(chip - relays[r] + chips, chips)
        distance = jnp.minimum(ahead, chips - ahead)
        cp = remote(own_m, gath.at[me], send_sem.at[r], chunk_sem.at[distance], device)
        return me != device, cp

    def send_to(which):
        for r in which:
            other, cp = to_relay(r)
            pl.when(other)(cp.start)

    pl.semaphore_wait(
        barrier,
        count + has_left.astype(jnp.int32) + has_right.astype(jnp.int32) - is_relay.astype(jnp.int32),
    )
    rows_to = remote(own_rows, cpl_v.at[place], send_sem.at[count], row_sem, my_relay)
    pl.when(jnp.logical_not(is_relay))(rows_to.start)
    send_to(range(FIRST))
    pl.when(has_right)(up.start)
    pl.when(has_left)(down.start)
    send_to(range(FIRST, count))

    def prepare(n):
        gath[me] = own_m[...]
        acc[...] = jnp.zeros(acc.shape, jnp.float32)
        cpl_v[place] = own_rows[...]
        others = cpl_v.at[pl.ds(0, n - 1)]
        remote(others, others, send_sem.at[0], row_sem, me).wait_recv()
        table = pltpu.make_async_copy(cpl_v, cpl, cpl_sem)
        table.start()
        table.wait()

    @pl.when(jnp.logical_and(is_relay, in_first))
    def _():
        prepare(first_served)

    pltpu.make_async_copy(near_hbm, near_v, near_sem).wait()

    @pl.when(has_left)
    def _():
        up.wait_recv()

    @pl.when(has_right)
    def _():
        down.wait_recv()

    @pl.when(jnp.logical_not(has_left))
    def _():
        ext[pl.ds(0, reach)] = jnp.zeros((reach, rhs, width), jnp.bfloat16)

    @pl.when(jnp.logical_not(has_right))
    def _():
        ext[pl.ds(reach + blocks, reach)] = jnp.zeros((reach, rhs, width), jnp.bfloat16)

    def near_block(b, carry):
        picked = []
        for j in range(slots):
            where = nbr[j, b] - (me * blocks - reach)
            where = jnp.minimum(jnp.maximum(where, 0), 2 * blocks - 1)
            picked.append(jnp.where(j < cnt[b], ext[where], zero))
        value = jnp.zeros((rhs, width), jnp.float32)
        for j in range(0, slots, 2):
            lhs = jnp.concatenate([picked[j], picked[j + 1]], axis=1)
            weights = jnp.concatenate([near_v[b, j], near_v[b, j + 1]], axis=1)
            value += lax.dot_general(lhs, weights, NT, preferred_element_type=jnp.float32)
        nearf[b] = value
        return carry

    lax.fori_loop(0, blocks, near_block, 0, unroll=2)
    @pl.when(jnp.logical_and(is_relay, in_second))
    def _():
        prepare(second_served)

    load_eva.wait()


    def give(at):
        device = (at // 2 * stride + chip) * 2 + at % 2
        return remote(loc_out.at[at], loc, result_sem, loc_sem, device)

    last = lax.rem(chip + chips // 2, chips)

    def moments_of(slot):
        return [gath[2 * slot + q // 2, q % 2].astype(jnp.float32) for q in range(4)]

    def add(at, sources):
        values = []
        for c in range(2):
            value = acc[at, c]
            for slot, moments in sources:
                for q in range(4):
                    value += cpl[at, c, 4 * slot + q] * moments[q]
            values.append(value)
        return values

    def result(at, sources):
        values = add(at, sources)
        for c in range(2):
            loc_out[at, c] = values[c].astype(jnp.bfloat16)

    @pl.when(jnp.logical_not(is_relay))
    def _():
        remote(loc, loc, send_sem.at[0], loc_sem, me).wait_recv()

    @pl.when(is_relay)
    def _():
        def arrive(distance, number):
            ref = gath.at[pl.ds(0, number)]
            remote(ref, ref, send_sem.at[0], chunk_sem.at[distance], me).wait_recv()

        def take(slots_in):
            sources = [(slot, moments_of(slot)) for slot in slots_in]

            def inner(k, carry):
                for at in [AT * k + n for n in range(AT)]:
                    values = add(at, sources)
                    acc[at, 0] = values[0]
                    acc[at, 1] = values[1]
                return carry

            lax.fori_loop(0, served // AT, inner, 0)

        arrive(0, 1)
        take([chip])

        def both(d, carry):
            arrive(d, 4)
            take([lax.rem(chip + d, chips), lax.rem(chip - d + chips, chips)])
            return carry

        lax.fori_loop(1, chips // 2, both, 0)
        arrive(chips // 2, 2)
        sources = [(last, moments_of(last))]
        result(0, sources)
        give(0).start()
        result(1, sources)
        loc[...] = loc_out[1]

    one = loc[0]
    two = loc[1]
    stores = []
    for i in range(2):
        for b in range(i * per, (i + 1) * per):
            lhs = jnp.where(cmap[b] == 2 * me, one, two)
            far = lax.dot_general(lhs, eva_v[b], NN, preferred_element_type=jnp.float32)
            out_v[b] = (nearf[b] + far).astype(jnp.bfloat16)
        piece = pl.ds(i * per, per)
        stores.append(pltpu.make_async_copy(out_v.at[piece], out_hbm.at[piece], out_sem.at[i]))
        stores[i].start()

    @pl.when(is_relay)
    def _():
        sources = [(last, moments_of(last))]

        def rest(k, carry):
            for at in (2 * k, 2 * k + 1):
                result(at, sources)
                give(at).start()
            return carry

        lax.fori_loop(1, served // 2, rest, 0)

    for chosen, n in ((in_first, first_served), (in_second, second_served)):
        @pl.when(jnp.logical_and(is_relay, chosen))
        def _():
            ref = loc_out.at[pl.ds(0, n - 1)]
            remote(ref, ref, result_sem, loc_sem, me).wait_send()

    for r in range(count):
        other, cp = to_relay(r)
        pl.when(other)(cp.wait_send)
    pl.when(jnp.logical_not(is_relay))(rows_to.wait_send)
    pl.when(has_right)(up.wait_send)
    pl.when(has_left)(down.wait_send)
    for cp in stores:
        cp.wait()


def shards(size, density, near_blocks, neighbours, counts, coarse_map, restrict, evaluate, coupling):
    blocks, rhs, width = density.shape
    slots = neighbours.shape[1]
    terms = restrict.shape[1]
    chips = size // 2
    served = 2 * (chips - chips // 4) // SECOND
    count = FIRST + SECOND
    bf16, f32 = jnp.bfloat16, jnp.float32
    dma = pltpu.SemaphoreType.DMA
    anywhere = pl.BlockSpec(memory_space=pl.ANY)
    return pl.pallas_call(
        functools.partial(kernel, size),
        out_shape=jax.ShapeDtypeStruct(density.shape, bf16),
        in_specs=[anywhere] * 8,
        out_specs=anywhere,
        scratch_shapes=[
            pltpu.SMEM((slots, blocks), jnp.int32),
            pltpu.SMEM((blocks,), jnp.int32),
            pltpu.SMEM((blocks,), jnp.int32),
            pltpu.SMEM((served, 2, 2 * size), f32),
            pltpu.VMEM((2 * blocks, rhs, width), bf16),
            pltpu.VMEM(near_blocks.shape, bf16),
            pltpu.VMEM(restrict.shape, bf16),
            pltpu.VMEM(evaluate.shape, bf16),
            pltpu.VMEM((blocks, rhs, width), f32),
            pltpu.VMEM((blocks, rhs, width), bf16),
            pltpu.VMEM((size, 2, rhs, terms), bf16),
            pltpu.VMEM((2, rhs, terms), bf16),
            pltpu.VMEM((2, 2 * size), f32),
            pltpu.VMEM((served, 2, 2 * size), f32),
            pltpu.VMEM((served, 2, rhs, terms), f32),
            pltpu.VMEM((2, rhs, terms), bf16),
            pltpu.VMEM((served, 2, rhs, terms), bf16),
            dma((4,)),
            dma,
            dma((2,)),
            dma,
            dma,
            dma((2,)),
            dma,
            dma((count + 3,)),
            dma((chips // 2 + 1,)),
            dma,
            dma((2,)),
            dma,
            dma,
        ],
        compiler_params=pltpu.CompilerParams(
            collective_id=0, has_side_effects=True, vmem_limit_bytes=67043328
        ),
        name="operator",
    )(neighbours.T, counts, coarse_map, coupling, density, near_blocks, restrict, evaluate)


def solution(mesh):
    placed = (
        P(GRP_PANEL, None, None),
        P(GRP_PANEL, None, None, None),
        P(GRP_PANEL, None),
        P(GRP_PANEL),
        P(GRP_PANEL),
        P(GRP_PANEL, None, None),
        P(GRP_PANEL, None, None),
        P(GRP_PANEL, None),
    )
    return jax.shard_map(
        functools.partial(shards, mesh.shape["panel"]),
        mesh=mesh,
        in_specs=placed,
        out_specs=P(GRP_PANEL, None, None),
        check_vma=False,
    )
```

time: 39.8 us -> 38.2 us (0.960)
  Pallas kernels: 37.7 us -> 36.5 us
    pallas_call x1, Pallas kernels: 37.7 us -> 36.5 us  [shards(): pl.pallas_call(functools.partial(kernel, size), out_shape=jax.ShapeDtypeS...]
where the time goes in v1:
time: 38.2 us; the launch traced here: 38 us
  Pallas kernels  36.5 us (96%)
  local copies, waits for them, and re-layouts  1.57 us (4%)
    pallas_call x1, Pallas kernels, shards(): pl.pallas_call(functools.partial(kernel, size), out_shape=jax.ShapeDtypeS...  36.5 us
    unnamed x1, local copies, waits for them, and re-layouts  1.57 us

profile of v1, /device:TPU:37, one launch (start us, length us, event | category | flops | bytes accessed | tf_op | source)
XLA Modules:
  0.0 38.0 jit_solution(7263147194875560730)
XLA Ops:
  0.0 36.5 %operator.1 = bf16[32,16,128]{2,1,0:T(8,128)(2,1)} custom-call(s32[8,32]{1,0:T(8,128)} %bitcast.1, s32[32]{0:T(128)} %cnt_hbm.1, s32[32]{0:T(128)} %map_hbm.1, f32[2,128]{1,0:T(2,128)} %cpl_hbm.1, bf16[32,16,128]{2,1,0:T(8,128)(2,1)} %dens_hbm.1, bf16[32,8,128,128]{3,2,1,0:T(8,128)(2,1)} %near_hbm.1, bf16[32,128,128]{2,1,0:T(8,128)(2,1)} %res_hbm.1, ...), custom_call_target="tpu_custom_call" | custom-call | tf_op jit(solution)/shard_map/operator/pallas_call | solution.py:372
  36.5 1.6 %copy.10 = bf16[32,16,128]{2,1,0:T(8,128)(2,1)} copy(bf16[32,16,128]{2,1,0:T(8,128)(2,1)} %operator.1) | data formatting | bytes 262144

commit v2 on v1

--- a/solution.py
+++ b/solution.py
@@ -145,22 +145,24 @@
     for cp in small:
         cp.wait()
     load_dens.wait()
-    total = jnp.zeros((2 * rhs, width), jnp.float32)
     zero = jnp.zeros((rhs, width), jnp.bfloat16)
 
-    def add_moments(total, first, last):
-        rows = []
-        for c in range(2):
-            rows.append(
-                jnp.concatenate(
-                    [jnp.where(cmap[b] == 2 * me + c, ext[reach + b], zero) for b in range(first, last)],
-                    axis=1,
+    def add_moments():
+        sums = []
+        quarter = blocks // 4
+        for first in range(0, blocks, quarter):
+            span = range(first, first + quarter)
+            rows = []
+            for c in range(2):
+                rows.append(
+                    jnp.concatenate(
+                        [jnp.where(cmap[b] == 2 * me + c, ext[reach + b], zero) for b in span], axis=1
+                    )
                 )
-            )
-        lhs = jnp.concatenate(rows, axis=0)
-        weights = jnp.concatenate([res_v[b] for b in range(first, last)], axis=1)
-        total += lax.dot_general(lhs, weights, NT, preferred_element_type=jnp.float32)
-        return total
+            lhs = jnp.concatenate(rows, axis=0)
+            weights = jnp.concatenate([res_v[b] for b in span], axis=1)
+            sums.append(lax.dot_general(lhs, weights, NT, preferred_element_type=jnp.float32))
+        return (sums[0] + sums[1]) + (sums[2] + sums[3])
 
     low_halo = ext.at[pl.ds(0, reach)]
     high_halo = ext.at[pl.ds(reach + blocks, reach)]
@@ -169,12 +171,11 @@
     up = remote(last_rows, low_halo, send_sem.at[count + 1], halo_sem.at[0], me + 1)
     down = remote(first_rows, high_halo, send_sem.at[count + 2], halo_sem.at[1], me - 1)
 
-    load_res[0].wait()
+    for cp in load_res:
+        cp.wait()
     for cp in load_near[:2]:
         cp.start()
-    total = add_moments(total, 0, per)
-    load_res[1].wait()
-    total = add_moments(total, per, blocks)
+    total = add_moments()
     own_m[...] = total.astype(jnp.bfloat16).reshape(2, rhs, width)
     for cp in load_near[2:]:
         cp.start()
@@ -319,6 +320,25 @@
         result(1, sources)
         loc[...] = loc_out[1]
 
+        @pl.when(in_first)
+        def _():
+            for at in range(2, first_served):
+                result(at, sources)
+                give(at).start()
+
+        @pl.when(in_second)
+        def _():
+            others = second_served // 2 - 1
+
+            def rest(i, carry):
+                k = 1 + lax.rem(i + others // 2, others)
+                for at in (2 * k, 2 * k + 1):
+                    result(at, sources)
+                    give(at).start()
+                return carry
+
+            lax.fori_loop(0, others, rest, 0)
+
     one = loc[0]
     two = loc[1]
     stores = []
@@ -330,18 +350,6 @@
         piece = pl.ds(i * per, per)
         stores.append(pltpu.make_async_copy(out_v.at[piece], out_hbm.at[piece], out_sem.at[i]))
         stores[i].start()
-
-    @pl.when(is_relay)
-    def _():
-        sources = [(last, moments_of(last))]
-
-        def rest(k, carry):
-            for at in (2 * k, 2 * k + 1):
-                result(at, sources)
-                give(at).start()
-            return carry
-
-        lax.fori_loop(1, served // 2, rest, 0)
 
     for chosen, n in ((in_first, first_served), (in_second, second_served)):
         @pl.when(jnp.logical_and(is_relay, chosen))

time: 38.2 us -> 37.8 us (0.990)
  Pallas kernels: 36.5 us -> 36 us
    pallas_call x1, Pallas kernels: 36.5 us -> 36 us  [shards(): pl.pallas_call(functools.partial(kernel, size), out_shape=jax.ShapeDtypeS...]
where the time goes in v2:
time: 37.8 us; the launch traced here: 37.6 us
  Pallas kernels  36 us (95%)
  local copies, waits for them, and re-layouts  1.57 us (4%)
    pallas_call x1, Pallas kernels, shards(): pl.pallas_call(functools.partial(kernel, size), out_shape=jax.ShapeDtypeS...  36 us
    unnamed x1, local copies, waits for them, and re-layouts  1.57 us

profile of v2, /device:TPU:37, one launch (start us, length us, event | category | flops | bytes accessed | tf_op | source)
XLA Modules:
  0.0 37.6 jit_solution(4418888050996252929)
XLA Ops:
  0.0 36.0 %operator.1 = bf16[32,16,128]{2,1,0:T(8,128)(2,1)} custom-call(s32[8,32]{1,0:T(8,128)} %bitcast.1, s32[32]{0:T(128)} %cnt_hbm.1, s32[32]{0:T(128)} %map_hbm.1, f32[2,128]{1,0:T(2,128)} %cpl_hbm.1, bf16[32,16,128]{2,1,0:T(8,128)(2,1)} %dens_hbm.1, bf16[32,8,128,128]{3,2,1,0:T(8,128)(2,1)} %near_hbm.1, bf16[32,128,128]{2,1,0:T(8,128)(2,1)} %res_hbm.1, ...), custom_call_target="tpu_custom_call" | custom-call | tf_op jit(solution)/shard_map/operator/pallas_call | solution.py:380
  36.1 1.6 %copy.10 = bf16[32,16,128]{2,1,0:T(8,128)(2,1)} copy(bf16[32,16,128]{2,1,0:T(8,128)(2,1)} %operator.1) | data formatting | bytes 262144
